TPU v7x, 256 devices: a whole 4x4x8 slice. The times are simulated.
256 devices in a mesh: dp: 32 (over y, x, core), mp: 8 (over z).
Axes of the slice: x: 4, y: 4, z: 8, core: 2. Of those that a mesh axis runs over, the one named last changes fastest.
Arguments:
- ref_hidden: bfloat16 [2048, 2048], P('dp', 'mp'), may hold values from -80 to 80
- proxy_hidden: bfloat16 [2048, 2048], P('dp', 'mp'), may hold values from -80 to 80
- ref_gain: float32 [2048], replicated, may hold values from 0.5 to 1.5
- proxy_gain: float32 [2048], replicated, may hold values from 0.5 to 1.5
- ref_head: bfloat16 [2048, 128256], P(None, ('dp', 'mp')), may hold values from -16 to 16
- proxy_head: bfloat16 [2048, 128256], P(None, ('dp', 'mp')), may hold values from -16 to 16
- token_ids: int32 [2048], P('dp'), may hold values from 0 to 128255
- bucket_ids: int32 [2048], P(('dp', 'mp')), may hold values from 0 to 4095
- domain_of_bucket: int32 [4096], replicated, may hold values from 0 to 21
- prior_weights: float32 [22], replicated, may hold values from 0.01 to 0.1
Outputs:
- ref_loss: float32 [2048], P(('dp', 'mp'))
- proxy_loss: float32 [2048], P(('dp', 'mp'))
- bucket_excess: float32 [4096], P(('dp', 'mp'))
- domain_log_weights: float32 [22], replicated
All inputs are finite; a program needn't handle non-finite values.
Results may differ from a plain program's by a relative error of at most 0.0035.
Values may be sent and summed in bfloat16 or wider, within the bound.
A program may use at most 64 MiB of HBM per device.

v0:
```python
import jax
import jax.numpy as jnp
from jax import lax
from jax.sharding import Mesh
from jax.sharding import PartitionSpec as P

DP_MP = ("dp_0", "dp_1", "dp_2", "mp")
DP = ("dp_0", "dp_1", "dp_2")


def in_one_piece(arrays, axis, dim, along):
    widths = [a.shape[along] for a in arrays]
    both = jnp.concatenate(arrays, axis=along)
    filled = lax.all_gather(both, axis, axis=dim, tiled=True)
    return tuple(jnp.split(filled, [sum(widths[:k]) for k in range(1, len(widths))], axis=along))


def gathered_once(x, axis):
    leaves = jax.tree.leaves(x)
    order = sorted(range(len(leaves)), key=lambda k: -leaves[k].size)
    width = (1, *leaves[order[0]].shape)[-1]
    lines = [
        jnp.pad(leaves[k].reshape(-1), (0, -leaves[k].size % width)).reshape(-1, width)
        for k in order
    ]
    both, at, found = (lax.all_gather(jnp.concatenate(lines), axis), 0, {})
    for k, line in zip(order, lines):
        piece = both[:, at : at + len(line)].reshape(len(both), -1)
        found[k] = piece[:, : leaves[k].size].reshape(-1, *leaves[k].shape)
        at += len(line)
    numbers = iter(range(len(leaves)))
    return jax.tree.map(lambda _: found[next(numbers)], x)


def merged_by_axis(x, axes, combine):
    for axis in axes:
        pieces = gathered_once(x, axis)
        x = jax.tree.map(lambda part: part[0], pieces)
        for k in range(1, lax.axis_size(axis)):
            x = combine(x, jax.tree.map(lambda part: part[k], pieces))
    return x


def over_axes(x, axes):
    for axis in axes:
        x = lax.psum(x, axis)
    return x


def normalize(hidden, gain):
    values = hidden.astype(jnp.float32)
    scale = lax.rsqrt(jnp.mean(values * values, -1, keepdims=True) + 1e-05)
    return (values * scale * gain).astype(jnp.bfloat16)


def row_stats(normed, targets, head, offset):
    logits = jnp.dot(normed, head, preferred_element_type=jnp.float32)
    top = jnp.max(logits, -1)
    total = jnp.sum(jnp.exp(logits - top[:, None]), -1)
    columns = lax.broadcasted_iota(jnp.int32, logits.shape, 1) + offset
    target = jnp.sum(jnp.where(columns == targets[:, None], logits, 0.0), -1)
    return (top, total, target)


def both_stats(norm_ref, norm_proxy, targets, ref_head, proxy_head, offset):
    first = row_stats(norm_ref, targets, ref_head, offset)
    second = row_stats(norm_proxy, targets, proxy_head, offset)
    return tuple((jnp.stack([left, right]) for left, right in zip(first, second)))


def combine_rows(earlier, later):
    top = jnp.maximum(earlier[0], later[0])
    total = earlier[1] * jnp.exp(earlier[0] - top) + later[1] * jnp.exp(later[0] - top)
    return (top, total, earlier[2] + later[2])


def on_device(
    ref_hidden,
    proxy_hidden,
    ref_gain,
    proxy_gain,
    ref_head,
    proxy_head,
    token_ids,
    bucket_ids,
    domain_of_bucket,
    prior_weights,
):
    vocab_dev = ref_head.shape[1]
    device = lax.axis_index(DP_MP)
    offset = device * vocab_dev
    own_rows = bucket_ids.shape[0]
    full_ref, full_proxy = in_one_piece((ref_hidden, proxy_hidden), "mp", 1, 0)
    norm_ref = normalize(full_ref, ref_gain)
    norm_proxy = normalize(full_proxy, proxy_gain)
    piece = (
        *in_one_piece((norm_ref, norm_proxy), DP, 0, 1),
        lax.all_gather(token_ids, DP, axis=0, tiled=True),
    )
    stats = both_stats(piece[0], piece[1], piece[2], ref_head, proxy_head, offset)
    top, total, target = tuple((fresh for fresh in stats))
    first_row = device * own_rows
    whole_top, whole_total, whole_target = merged_by_axis((top, total, target), DP_MP, combine_rows)
    own_top = lax.dynamic_slice_in_dim(whole_top, first_row, own_rows, 1)
    own_total = lax.dynamic_slice_in_dim(whole_total, first_row, own_rows, 1)
    own_target = lax.dynamic_slice_in_dim(whole_target, first_row, own_rows, 1)
    losses = own_top + jnp.log(own_total) - own_target
    excess = jnp.maximum(losses[1] - losses[0], 0.0)
    buckets = domain_of_bucket.shape[0]
    domains = prior_weights.shape[0]
    onehot = (bucket_ids[:, None] == lax.broadcasted_iota(jnp.int32, (1, buckets), 1)).astype(
        jnp.float32
    )
    table = jnp.dot(
        jnp.stack([excess, jnp.ones_like(excess)]),
        onehot,
        precision=lax.Precision.HIGHEST,
        preferred_element_type=jnp.float32,
    )
    domain_hot = (
        domain_of_bucket[:, None] == lax.broadcasted_iota(jnp.int32, (1, domains), 1)
    ).astype(jnp.float32)
    bucket_dev = buckets // lax.axis_size(DP_MP)
    first_bucket = device * bucket_dev
    full_table = over_axes(table, DP_MP)
    domain_totals = jnp.dot(
        full_table, domain_hot, precision=lax.Precision.HIGHEST, preferred_element_type=jnp.float32
    )
    own_table = lax.dynamic_slice_in_dim(full_table, first_bucket, bucket_dev, 1)
    bucket_excess = own_table[0] / jnp.maximum(own_table[1], 1.0)
    domain_excess = domain_totals[0] / jnp.maximum(domain_totals[1], 1.0)
    weights = jax.nn.softmax(jnp.log(prior_weights) + 1.0 * domain_excess)
    domain_log_weights = jnp.log(0.999 * weights + 0.001 / domains)
    return (losses[0], losses[1], bucket_excess, domain_log_weights)


def solution(mesh):
    torus = Mesh(mesh.devices.reshape(4, 4, 2, mesh.shape["mp"]), ("dp_0", "dp_1", "dp_2", "mp"))
    return jax.shard_map(
        on_device,
        mesh=torus,
        in_specs=(
            P(DP, "mp"),
            P(DP, "mp"),
            P(),
            P(),
            P(None, DP_MP),
            P(None, DP_MP),
            P(DP),
            P(DP_MP),
            P(),
            P(),
        ),
        out_specs=(P(DP_MP), P(DP_MP), P(DP_MP), P()),
        check_vma=False,
    )
```

profile of v0, /device:TPU:8, one launch (start us, length us, event | category | flops | bytes accessed | tf_op | source)
XLA Modules:
  0.0 261.2 jit_solution(11383560652746233583)
XLA Ops:
  7.2 0.0 copy-start
  7.2 0.0 all-gather.10.cloned.1.call-start
  7.2 0.9 pad_maximum_fusion.1
  8.1 29.1 %all_gather.33 = bf16[128,2048]{1,0:T(8,128)(2,1)S(1)} all-gather(bf16[128,256]{1,0:T(8,128)(2,1)S(1)} %pad_maximum_fusion.1), channel_id=1, replica_groups=mesh['dp_0'=4,'dp_1'=4,'dp_2'=2,'mp'=8] {'mp'}, dimensions={1}, use_global_device_ids=true | all-gather | bytes 589824 | tf_op jit(solution)/shard_map/all_gather | solution.py:14
  37.3 0.2 fusion.6
  37.5 0.9 fusion.8
  38.4 0.8 pad_maximum_fusion
  39.2 0.0 all-gather.10.cloned.1.call-update
  39.2 1.3 dynamic-slice.1
  41.2 0.9 dynamic-update-slice
  42.0 15.8 %all-reduce.1 = s32[2048]{0:T(1024)S(1)} all-reduce(s32[2048]{0:T(1024)S(1)} %dynamic-update-slice), channel_id=1, replica_groups=mesh['dp_0'=4,'dp_1'=4,'dp_2'=2,'mp'=8] {'dp_0','dp_1','dp_2'}, use_global_device_ids=true, to_apply=%add.1 | all-reduce | flops 2048 | bytes 16384
  57.8 57.8 %all-gather.10.cloned.1.call-done = bf16[2048,4096]{1,0:T(8,128)(2,1)} async-done(((bf16[64,4096]{1,0:T(8,128)(2,1)}), bf16[2048,4096]{1,0:T(8,128)(2,1)}) %all-gather.10.cloned.1.call-update) | async-done | bytes 16777232 | tf_op jit(solution)/shard_map/all_gather | solution.py:14
  115.6 0.0 copy-done
  115.6 0.0 copy-start.2
  115.6 0.0 copy-start.3
  115.7 7.1 %fusion.103 = (f32[2048]{0:T(1024)S(1)}, f32[2048,501]{0,1:T(8,128)S(1)}) fusion(bf16[2048,501]{0,1:T(8,128)(2,1)S(1)} %copy-done, bf16[2048,4096]{1,0:T(8,128)(2,1)} %all-gather.10.cloned.1.call-done), kind=kOutput, calls=%fused_computation.188 | convolution fusion | flops 4203716608 | bytes 14553088 | tf_op jit(solution)/shard_map/dot_general | solution.py:57
  122.7 1.2 copy-done.2
  123.9 0.6 copy-done.3
  124.5 4.5 %fusion.104 = (f32[2048]{0:T(1024)S(1)}, f32[2048,501]{0,1:T(8,128)S(1)}) fusion(bf16[2048,501]{0,1:T(8,128)(2,1)S(1)} %copy-done.3, bf16[2048,4096]{1,0:T(8,128)(2,1)S(1)} %copy-done.2), kind=kOutput, calls=%fused_computation.189 | convolution fusion | flops 4203716608 | bytes 14565376 | tf_op jit(solution)/shard_map/dot_general | solution.py:57
  129.0 0.0 copy-start.5
  129.0 0.0 copy-start.4
  129.0 0.0 copy-start.1
  129.0 2.1 fusion.5
  131.2 0.1 concatenate.21
  131.2 12.6 %all-gather.4 = f32[4,6,2048]{2,1,0:T(8,128)S(1)} all-gather(f32[1,6,2048]{2,1,0:T(8,128)S(1)} %bitcast.321), channel_id=2, replica_groups=mesh['dp_0'=4,'dp_1'=4,'dp_2'=2,'mp'=8] {'dp_0'}, dimensions={0}, use_global_device_ids=true | all-gather | bytes 245760 | tf_op jit(solution)/shard_map/all_gather | solution.py:26
  143.8 0.1 fusion.44
  144.0 12.3 %all-gather.5 = f32[4,6,2048]{2,1,0:T(8,128)S(1)} all-gather(f32[1,6,2048]{2,1,0:T(8,128)S(1)} %maximum_bitcast_fusion), channel_id=3, replica_groups=mesh['dp_0'=4,'dp_1'=4,'dp_2'=2,'mp'=8] {'dp_1'}, dimensions={0}, use_global_device_ids=true | all-gather | bytes 245760 | tf_op jit(solution)/shard_map/all_gather | solution.py:26
  156.2 0.1 fusion.34
  156.4 1.9 all-gather.6
  158.4 27.0 %all-gather.7 = f32[8,6,2048]{2,1,0:T(8,128)S(1)} all-gather(f32[1,6,2048]{2,1,0:T(8,128)S(1)} %maximum_bitcast_fusion.2), channel_id=5, replica_groups=mesh['dp_0'=4,'dp_1'=4,'dp_2'=2,'mp'=8] {'mp'}, dimensions={0}, use_global_device_ids=true | all-gather | bytes 442368 | tf_op jit(solution)/shard_map/all_gather | solution.py:26
  185.5 0.1 fusion.102
  185.6 0.1 subtract_exponential_fusion
  185.7 0.1 fusion.68
  185.8 0.5 subtract_maximum_fusion
  186.4 0.0 copy-done.5
  186.4 0.3 fusion.14
  186.6 14.4 %psum.28 = f32[2,4096]{1,0:T(2,128)S(1)} all-reduce(f32[2,4096]{1,0:T(2,128)S(1)} %fusion.14), channel_id=1, replica_groups=mesh['dp_0'=4,'dp_1'=4,'dp_2'=2,'mp'=8] {'dp_0'}, use_global_device_ids=true, to_apply=%region_8.9 | all-reduce | flops 8192 | bytes 65536 | tf_op jit(solution)/shard_map/psum | solution.py:46
  201.0 16.7 %psum.29 = f32[2,4096]{1,0:T(2,128)S(1)} all-reduce(f32[2,4096]{1,0:T(2,128)S(1)} %psum.28), channel_id=1, replica_groups=mesh['dp_0'=4,'dp_1'=4,'dp_2'=2,'mp'=8] {'dp_1'}, use_global_device_ids=true, to_apply=%region_9.10 | all-reduce | flops 8192 | bytes 65536 | tf_op jit(solution)/shard_map/psum | solution.py:46
  217.7 3.4 %psum.30 = f32[2,4096]{1,0:T(2,128)S(1)} all-reduce(f32[2,4096]{1,0:T(2,128)S(1)} %psum.29), channel_id=1, replica_groups=mesh['dp_0'=4,'dp_1'=4,'dp_2'=2,'mp'=8] {'dp_2'}, use_global_device_ids=true, to_apply=%region_10.11 | all-reduce | flops 8192 | bytes 65536 | tf_op jit(solution)/shard_map/psum | solution.py:46
  221.1 28.5 %psum.31 = f32[2,4096]{1,0:T(2,128)S(1)} all-reduce(f32[2,4096]{1,0:T(2,128)S(1)} %psum.30), channel_id=1, replica_groups=mesh['dp_0'=4,'dp_1'=4,'dp_2'=2,'mp'=8] {'mp'}, use_global_device_ids=true, to_apply=%region_11.12 | all-reduce | flops 8192 | bytes 65536 | tf_op jit(solution)/shard_map/psum | solution.py:46
  249.6 0.0 copy-done.4
  249.6 0.3 fusion.12
  249.9 0.0 copy-done.1
  249.9 0.6 fusion.95
  250.5 1.3 fusion.92
  251.8 1.9 add_log_fusion
  253.7 0.1 constant_dynamic-slice_fusion.15
  253.8 0.5 fusion.90
  (11 shorter events, 0.3 us)
Async XLA Ops:
  7.2 108.5 %copy-start = (bf16[2048,501]{0,1:T(8,128)(2,1)S(1)}, bf16[2048,501]{0,1:T(8,128)(2,1)}, u32[]{:S(2)}) copy-start(bf16[2048,501]{0,1:T(8,128)(2,1)} %param.14) | copy-start | bytes 6156292
  7.2 108.5 %all-gather.10.cloned.1.call-start = ((), (), s32[]{:S(2)}) async-start(), calls=%async_computation | async-start | bytes 17301504 | tf_op jit(solution)/shard_map/all_gather | solution.py:14
  115.6 8.2 %copy-start.2 = (bf16[2048,4096]{1,0:T(8,128)(2,1)S(1)}, bf16[2048,4096]{1,0:T(8,128)(2,1)}, u32[]{:S(2)}) copy-start(bf16[2048,4096]{1,0:T(8,128)(2,1)} %all-gather.10.cloned.1.call-done) | copy-start | bytes 50331652
  115.6 8.8 %copy-start.3 = (bf16[2048,501]{0,1:T(8,128)(2,1)S(1)}, bf16[2048,501]{0,1:T(8,128)(2,1)}, u32[]{:S(2)}) copy-start(bf16[2048,501]{0,1:T(8,128)(2,1)} %param.15) | copy-start | bytes 6156292
  129.0 57.4 %copy-start.5 = (s32[8]{0:T(128)S(1)}, s32[8]{0:T(128)}, u32[]{:S(2)}) copy-start(s32[8]{0:T(128)} %param.17) | copy-start | bytes 100
  129.0 120.6 %copy-start.4 = (s32[4096]{0:T(1024)S(1)}, s32[4096]{0:T(1024)}, u32[]{:S(2)}) copy-start(s32[4096]{0:T(1024)} %param.18) | copy-start | bytes 49156
  129.0 120.9 %copy-start.1 = (f32[22]{0:T(128)S(1)}, f32[22]{0:T(128)}, u32[]{:S(2)}) copy-start(f32[22]{0:T(128)} %param.19) | copy-start | bytes 268
Sparse Core Ops, SparseCore 0:
  39.4 76.2 all-gather.9
where the time goes:
time: 262 us; the launch traced here: 261 us
  blocking collectives  162 us (62%)
  waiting for transfers between devices  57.8 us (22%)
  between operations  14.9 us (6%)
  matrix products  12.1 us (5%)
  other arithmetic  10.6 us (4%)
  local copies, waits for them, and re-layouts  4.07 us (2%)
    psum x4, blocking collectives, over_axes(): x = lax.psum(x, axis)  62.9 us
    all_gather x1, waiting for transfers between devices, in_one_piece(): filled = lax.all_gather(both, axis, axis=dim, tiled=True)  57.8 us
    all_gather x4, blocking collectives, gathered_once(): both, at, found = (lax.all_gather(jnp.concatenate(lines), axis), 0, {})  53.8 us
    all_gather x1, blocking collectives, in_one_piece(): filled = lax.all_gather(both, axis, axis=dim, tiled=True)  29.1 us
    unnamed x1, blocking collectives  15.8 us
    dot_general x2, matrix products, row_stats(): logits = jnp.dot(normed, head, preferred_element_type=jnp.float32)  11.6 us
  transfers between devices with their start and end apart: 1, of which 1 were waited for; matrix products, arithmetic and copies ran while one was open for 1% of the time, Pallas kernels for 0%

commit v1 on v0

--- a/solution.py
+++ b/solution.py
@@ -6,6 +6,10 @@
 
 DP_MP = ("dp_0", "dp_1", "dp_2", "mp")
 DP = ("dp_0", "dp_1", "dp_2")
+
+
+def lay_the_routes_all(my_data, peer_axis):
+    return jax.lax.all_gather(my_data, peer_axis).sum(axis=0)
 
 
 def in_one_piece(arrays, axis, dim, along):
@@ -43,7 +47,7 @@
 
 def over_axes(x, axes):
     for axis in axes:
-        x = lax.psum(x, axis)
+        x = lay_the_routes_all(x, axis)
     return x
 
 

time: 262 us -> 250 us (0.954)
  blocking collectives: 162 us -> 149 us
    psum x4 -> x0, blocking collectives: 62.9 us -> none  [over_axes(): x = lax.psum(x, axis)]
    all_gather x0 -> x4, blocking collectives: none -> 50.6 us  [lay_the_routes_all(): return jax.lax.all_gather(my_data, peer_axis).sum(axis=0)]
where the time goes in v1:
time: 250 us; the launch traced here: 249 us
  blocking collectives  149 us (60%)
  waiting for transfers between devices  57.8 us (23%)
  between operations  14.9 us (6%)
  matrix products  12.1 us (5%)
  other arithmetic  10.9 us (4%)
  local copies, waits for them, and re-layouts  4.07 us (2%)
    all_gather x1, waiting for transfers between devices, in_one_piece(): filled = lax.all_gather(both, axis, axis=dim, tiled=True)  57.8 us
    all_gather x4, blocking collectives, gathered_once(): both, at, found = (lax.all_gather(jnp.concatenate(lines), axis), 0, {})  53.8 us
    all_gather x4, blocking collectives, lay_the_routes_all(): return jax.lax.all_gather(my_data, peer_axis).sum(axis=0)  50.6 us
    all_gather x1, blocking collectives, in_one_piece(): filled = lax.all_gather(both, axis, axis=dim, tiled=True)  29.1 us
    unnamed x1, blocking collectives  15.8 us
    dot_general x2, matrix products, row_stats(): logits = jnp.dot(normed, head, preferred_element_type=jnp.float32)  11.6 us
  transfers between devices with their start and end apart: 1, of which 1 were waited for; matrix products, arithmetic and copies ran while one was open for 1% of the time, Pallas kernels for 0%

profile of v1, /device:TPU:8, one launch (start us, length us, event | category | flops | bytes accessed | tf_op | source)
XLA Modules:
  0.0 249.1 jit_solution(4975252972946875192)
XLA Ops:
  7.2 0.0 copy-start
  7.2 0.0 all-gather.18.cloned.1.call-start
  7.2 0.9 pad_maximum_fusion.1
  8.1 29.1 %all_gather.57 = bf16[128,2048]{1,0:T(8,128)(2,1)S(1)} all-gather(bf16[128,256]{1,0:T(8,128)(2,1)S(1)} %pad_maximum_fusion.1), channel_id=1, replica_groups=mesh['dp_0'=4,'dp_1'=4,'dp_2'=2,'mp'=8] {'mp'}, dimensions={1}, use_global_device_ids=true | all-gather | bytes 589824 | tf_op jit(solution)/shard_map/all_gather | solution.py:18
  37.3 0.2 fusion.6
  37.5 0.9 fusion.8
  38.4 0.8 pad_maximum_fusion
  39.2 0.0 all-gather.18.cloned.1.call-update
  39.2 1.3 dynamic-slice.1
  41.2 0.9 dynamic-update-slice
  42.0 15.8 %all-reduce.1 = s32[2048]{0:T(1024)S(1)} all-reduce(s32[2048]{0:T(1024)S(1)} %dynamic-update-slice), channel_id=1, replica_groups=mesh['dp_0'=4,'dp_1'=4,'dp_2'=2,'mp'=8] {'dp_0','dp_1','dp_2'}, use_global_device_ids=true, to_apply=%add.1 | all-reduce | flops 2048 | bytes 16384
  57.8 57.8 %all-gather.18.cloned.1.call-done = bf16[2048,4096]{1,0:T(8,128)(2,1)} async-done(((bf16[64,4096]{1,0:T(8,128)(2,1)}), bf16[2048,4096]{1,0:T(8,128)(2,1)}) %all-gather.18.cloned.1.call-update) | async-done | bytes 16777232 | tf_op jit(solution)/shard_map/all_gather | solution.py:18
  115.6 0.0 copy-done
  115.6 0.0 copy-start.2
  115.6 0.0 copy-start.3
  115.7 7.1 %fusion.102 = (f32[2048]{0:T(1024)S(1)}, f32[2048,501]{0,1:T(8,128)S(1)}) fusion(bf16[2048,501]{0,1:T(8,128)(2,1)S(1)} %copy-done, bf16[2048,4096]{1,0:T(8,128)(2,1)} %all-gather.18.cloned.1.call-done), kind=kOutput, calls=%fused_computation.188 | convolution fusion | flops 4203716608 | bytes 14553088 | tf_op jit(solution)/shard_map/dot_general | solution.py:61
  122.7 1.2 copy-done.2
  123.9 0.6 copy-done.3
  124.5 4.5 %fusion.103 = (f32[2048]{0:T(1024)S(1)}, f32[2048,501]{0,1:T(8,128)S(1)}) fusion(bf16[2048,501]{0,1:T(8,128)(2,1)S(1)} %copy-done.3, bf16[2048,4096]{1,0:T(8,128)(2,1)S(1)} %copy-done.2), kind=kOutput, calls=%fused_computation.189 | convolution fusion | flops 4203716608 | bytes 14565376 | tf_op jit(solution)/shard_map/dot_general | solution.py:61
  129.0 0.0 copy-start.5
  129.0 2.1 fusion.5
  131.1 0.0 copy-start.4
  131.1 0.0 copy-start.1
  131.2 0.1 concatenate.21
  131.2 12.6 %all-gather.8 = f32[4,6,2048]{2,1,0:T(8,128)S(1)} all-gather(f32[1,6,2048]{2,1,0:T(8,128)S(1)} %bitcast.326), channel_id=2, replica_groups=mesh['dp_0'=4,'dp_1'=4,'dp_2'=2,'mp'=8] {'dp_0'}, dimensions={0}, use_global_device_ids=true | all-gather | bytes 245760 | tf_op jit(solution)/shard_map/all_gather | solution.py:30
  143.8 0.1 fusion.43
  144.0 12.3 %all-gather.9 = f32[4,6,2048]{2,1,0:T(8,128)S(1)} all-gather(f32[1,6,2048]{2,1,0:T(8,128)S(1)} %maximum_bitcast_fusion), channel_id=3, replica_groups=mesh['dp_0'=4,'dp_1'=4,'dp_2'=2,'mp'=8] {'dp_1'}, dimensions={0}, use_global_device_ids=true | all-gather | bytes 245760 | tf_op jit(solution)/shard_map/all_gather | solution.py:30
  156.2 0.1 fusion.33
  156.4 1.9 all-gather.10
  158.4 27.0 %all-gather.11 = f32[8,6,2048]{2,1,0:T(8,128)S(1)} all-gather(f32[1,6,2048]{2,1,0:T(8,128)S(1)} %maximum_bitcast_fusion.2), channel_id=5, replica_groups=mesh['dp_0'=4,'dp_1'=4,'dp_2'=2,'mp'=8] {'mp'}, dimensions={0}, use_global_device_ids=true | all-gather | bytes 442368 | tf_op jit(solution)/shard_map/all_gather | solution.py:30
  185.5 0.1 fusion.101
  185.6 0.1 subtract_exponential_fusion
  185.7 0.1 fusion.67
  185.8 0.5 subtract_maximum_fusion
  186.4 0.0 copy-done.5
  186.4 0.3 convolution_bitcast_fusion
  186.6 12.0 %all-gather.12 = f32[4,2,4096]{2,1,0:T(2,128)S(1)} all-gather(f32[1,2,4096]{2,1,0:T(2,128)S(1)} %convolution_bitcast_fusion), channel_id=6, replica_groups=mesh['dp_0'=4,'dp_1'=4,'dp_2'=2,'mp'=8] {'dp_0'}, dimensions={0}, use_global_device_ids=true | all-gather | bytes 163840 | tf_op jit(solution)/shard_map/all_gather | solution.py:12
  198.6 0.1 reduce_sum.105
  198.7 12.0 %all-gather.13 = f32[4,2,4096]{2,1,0:T(2,128)S(1)} all-gather(f32[1,2,4096]{2,1,0:T(2,128)S(1)} %bitcast.327), channel_id=7, replica_groups=mesh['dp_0'=4,'dp_1'=4,'dp_2'=2,'mp'=8] {'dp_1'}, dimensions={0}, use_global_device_ids=true | all-gather | bytes 163840 | tf_op jit(solution)/shard_map/all_gather | solution.py:12
  210.7 0.1 reduce_sum.106
  210.7 1.9 all-gather.14
  212.6 24.8 %all-gather.15 = f32[8,2,4096]{2,1,0:T(2,128)S(1)} all-gather(f32[1,2,4096]{2,1,0:T(2,128)S(1)} %bitcast.329), channel_id=9, replica_groups=mesh['dp_0'=4,'dp_1'=4,'dp_2'=2,'mp'=8] {'mp'}, dimensions={0}, use_global_device_ids=true | all-gather | bytes 294912 | tf_op jit(solution)/shard_map/all_gather | solution.py:12
  237.4 0.1 reduce_sum.108
  237.5 0.0 copy-done.4
  237.5 0.3 fusion.12
  237.8 0.0 copy-done.1
  237.8 0.6 fusion.94
  238.4 1.3 fusion.91
  239.8 1.9 add_log_fusion
  241.6 0.1 constant_dynamic-slice_fusion.15
  241.7 0.5 fusion.89
  (12 shorter events, 0.3 us)
Async XLA Ops:
  7.2 108.5 %copy-start = (bf16[2048,501]{0,1:T(8,128)(2,1)S(1)}, bf16[2048,501]{0,1:T(8,128)(2,1)}, u32[]{:S(2)}) copy-start(bf16[2048,501]{0,1:T(8,128)(2,1)} %param.14) | copy-start | bytes 6156292
  7.2 108.5 %all-gather.18.cloned.1.call-start = ((), (), s32[]{:S(2)}) async-start(), calls=%async_computation | async-start | bytes 17301504 | tf_op jit(solution)/shard_map/all_gather | solution.py:18
  115.6 8.2 %copy-start.2 = (bf16[2048,4096]{1,0:T(8,128)(2,1)S(1)}, bf16[2048,4096]{1,0:T(8,128)(2,1)}, u32[]{:S(2)}) copy-start(bf16[2048,4096]{1,0:T(8,128)(2,1)} %all-gather.18.cloned.1.call-done) | copy-start | bytes 50331652
  115.6 8.8 %copy-start.3 = (bf16[2048,501]{0,1:T(8,128)(2,1)S(1)}, bf16[2048,501]{0,1:T(8,128)(2,1)}, u32[]{:S(2)}) copy-start(bf16[2048,501]{0,1:T(8,128)(2,1)} %param.15) | copy-start | bytes 6156292
  129.0 57.4 %copy-start.5 = (s32[8]{0:T(128)S(1)}, s32[8]{0:T(128)}, u32[]{:S(2)}) copy-start(s32[8]{0:T(128)} %param.17) | copy-start | bytes 100
  131.1 106.4 %copy-start.4 = (s32[4096]{0:T(1024)S(1)}, s32[4096]{0:T(1024)}, u32[]{:S(2)}) copy-start(s32[4096]{0:T(1024)} %param.18) | copy-start | bytes 49156
  131.1 106.7 %copy-start.1 = (f32[22]{0:T(128)S(1)}, f32[22]{0:T(128)}, u32[]{:S(2)}) copy-start(f32[22]{0:T(128)} %param.19) | copy-start | bytes 268
Sparse Core Ops, SparseCore 0:
  39.4 76.2 all-gather.17
